TPU v7x, 128 devices: a whole 4x4x4 slice. The times are simulated.
128 devices in a mesh: atom: 32 (over y, z, core), aux: 4 (over x).
Axes of the slice: x: 4, y: 4, z: 4, core: 2. Of those that a mesh axis runs over, the one named last changes fastest.
Arguments:
- pao_blocks: bfloat16 [64, 24, 15360], P('atom', None, 'aux'), may hold values from -0.048339844 to 0.048339844
- cabs_blocks: bfloat16 [64, 48, 15360], P('atom', None, 'aux'), may hold values from -0.3046875 to 0.3046875
- cabs_weight: bfloat16 [64, 48], P('atom'), may hold values from 0.25 to 4
- pair_blocks: int32 [2048, 4], P('atom'), may hold values from 0 to 63, as said below
- pao_size: int32 [2048], P('atom'), may hold values from 24 to 96
- cabs_size: int32 [2048], P('atom'), may hold values from 48 to 192
Outputs:
- v_pairs: float32 [2048, 96, 96], P('atom', 'aux')
Inputs may be any that keep to these rules, and one draw needn't show every extreme that they name: `pair_blocks`: each row names 4 different atom blocks; atom block b belongs to owner b // 2, and the 64 rows of one index of atom name at most one block of each owner.
All inputs are finite; a program needn't handle non-finite values.
Results may differ from a plain program's by a relative error of at most 0.0003.
Values may be sent and summed in bfloat16 or wider, within the bound.
A program may use at most 128 MiB of HBM per device.

v0:
```python
import jax
import jax.numpy as jnp
from jax import lax
from jax.sharding import PartitionSpec as P


def sent_together(arrays, axis, dim, along):
    ends, at = ([], 0)
    for a in arrays[:-1]:
        at += a.shape[along]
        ends.append(at)
    both = jnp.concatenate(arrays, axis=along)
    return tuple(
        jnp.split(lax.psum_scatter(both, axis, scatter_dimension=dim, tiled=True), ends, axis=along)
    )


def collect(pieces):
    return (pieces[0], pieces[1], pieces[2])


def shards(pao_blocks, cabs_blocks, cabs_weight, pair_blocks, pao_size, cabs_size):
    owners = lax.axis_size("atom")
    blk_dev = pao_blocks.shape[0]
    pao_rows = pao_blocks.shape[1]
    cabs_rows = cabs_blocks.shape[1]
    aux_local = pao_blocks.shape[2]
    pair_count = pair_blocks.shape[0]
    dom_count = pair_blocks.shape[1]
    pao_width = dom_count * pao_rows
    cabs_width = dom_count * cabs_rows
    flat_blocks = pair_blocks.reshape(-1)
    owner_ids = flat_blocks // blk_dev
    owner_range = jnp.arange(owners, dtype=jnp.int32)
    matches = owner_ids[:, None] == owner_range[None, :]
    wanted = jnp.max(jnp.where(matches, flat_blocks[:, None], -1), axis=0)
    every_pao, every_cabs, every_weight = collect(
        (
            lax.all_gather(pao_blocks, "atom", axis=0, tiled=True),
            lax.all_gather(cabs_blocks, "atom", axis=0, tiled=True),
            lax.all_gather(cabs_weight, "atom", axis=0, tiled=True),
        )
    )
    chosen = jnp.maximum(wanted, 0)
    slot_pao = jnp.take(every_pao, chosen, axis=0)
    slot_cabs = jnp.take(every_cabs, chosen, axis=0)
    slot_weight = jnp.take(every_weight, chosen, axis=0)
    slot_of = owner_ids.reshape(pair_count, dom_count)
    group_size = 4
    groups = slot_of.reshape(pair_count // group_size, group_size, dom_count)

    def pair_products(slots):
        rows_pao = jnp.take(slot_pao, slots.reshape(-1), axis=0).reshape(
            group_size, pao_width, aux_local
        )
        rows_cabs = jnp.take(slot_cabs, slots.reshape(-1), axis=0).reshape(
            group_size, cabs_width, aux_local
        )
        margin_part = jnp.einsum(
            "pia,pja->pij", rows_pao, rows_pao, preferred_element_type=jnp.float32
        )
        coupling_part = jnp.einsum(
            "pia,pja->pij", rows_pao, rows_cabs, preferred_element_type=jnp.float32
        )
        return (margin_part, coupling_part)

    margin, coupling = lax.map(pair_products, groups)
    margin = margin.reshape(pair_count, pao_width, pao_width)
    coupling = coupling.reshape(pair_count, pao_width, cabs_width)
    keep_pao = (jnp.arange(pao_width, dtype=jnp.int32)[None, :] < pao_size[:, None]).astype(
        jnp.float32
    )
    keep_cabs = (jnp.arange(cabs_width, dtype=jnp.int32)[None, :] < cabs_size[:, None]).astype(
        jnp.float32
    )
    margin = margin * keep_pao[:, :, None] * keep_pao[:, None, :]
    coupling = coupling * keep_pao[:, :, None] * keep_cabs[:, None, :]
    scales = (
        jnp.take(slot_weight, slot_of.reshape(-1), axis=0)
        .reshape(pair_count, cabs_width)
        .astype(jnp.float32)
    )
    margin_rows, coupling_rows = sent_together((margin, coupling), "aux", 1, 2)
    coupling_full = lax.all_gather(coupling_rows, "aux", axis=1, tiled=True)
    return margin_rows - jnp.einsum(
        "pix,pjx->pij",
        coupling_rows * scales[:, None, :],
        coupling_full,
        precision=lax.Precision.HIGHEST,
    )


def solution(mesh):
    placed = (
        P("atom", None, "aux"),
        P("atom", None, "aux"),
        P("atom", None),
        P("atom", None),
        P("atom"),
        P("atom"),
    )
    return jax.shard_map(
        shards, mesh=mesh, in_specs=placed, out_specs=P("atom", "aux", None), check_vma=False
    )
```

profile of v0, /device:TPU:1, one launch (start us, length us, event | category | flops | bytes accessed | tf_op | source)
XLA Modules:
  0.0 740.0 jit_solution(4457633753350145893)
XLA Ops:
  10.6 63.6 %all-gather.5.cloned.1.call-done = bf16[64,24,3840]{2,1,0:T(8,128)(2,1)} async-done(((bf16[2,24,3840]{2,1,0:T(8,128)(2,1)}), bf16[64,24,3840]{2,1,0:T(8,128)(2,1)}) %all-gather.5.cloned.1.call-update) | async-done | bytes 11796496 | tf_op jit(solution)/shard_map/all_gather | solution.py:39
  74.3 7.9 %gather_fusion.2 = bf16[32,24,3840]{2,1,0:T(8,128)(2,1)} fusion(bf16[64,24,3840]{2,1,0:T(8,128)(2,1)} %all-gather.5.cloned.1.call-done, s32[1024]{0:T(1024)S(1)} %pad_clamp_fusion.2), kind=kCustom, calls=%fused_computation.2 | custom fusion | bytes 11796608 | tf_op jit(solution)/shard_map/jit(_take)/gather | solution.py:45
  82.1 5.9 broadcast_select_fusion.1
  88.0 76.2 %all-gather.7.cloned.1.call-done = bf16[64,48,3840]{2,1,0:T(8,128)(2,1)} async-done(((bf16[2,48,3840]{2,1,0:T(8,128)(2,1)}), bf16[64,48,3840]{2,1,0:T(8,128)(2,1)}) %all-gather.7.cloned.1.call-update) | async-done | bytes 23592976 | tf_op jit(solution)/shard_map/all_gather | solution.py:40
  164.2 14.1 %gather_fusion.3 = bf16[32,48,3840]{2,1,0:T(8,128)(2,1)} fusion(bf16[64,48,3840]{2,1,0:T(8,128)(2,1)} %all-gather.7.cloned.1.call-done, s32[1024]{0:T(1024)S(1)} %pad_clamp_fusion.2), kind=kCustom, calls=%fused_computation.3 | custom fusion | bytes 23593088 | tf_op jit(solution)/shard_map/jit(_take)/gather | solution.py:46
  178.4 10.3 %broadcast_select_fusion = bf16[32,48,3840]{2,1,0:T(8,128)(2,1)} fusion(bf16[32,48,3840]{2,1,0:T(8,128)(2,1)} %gather_fusion.3, pred[32]{0:T(512)(128)(4,1)S(1)} %broadcast_compare_fusion), kind=kLoop, calls=%fused_computation.18 | loop fusion | flops 5898240 | bytes 23592992 | tf_op jit(solution)/shard_map/jit(_take)/select_n | solution.py:46
  188.6 368.7 %while.12 = (s32[]{:T(128)}, f32[16,4,96,96]{3,2,1,0:T(8,128)}, f32[16,4,96,192]{3,2,1,0:T(8,128)}, s32[16,4,4]{2,1,0:T(4,128)S(1)}, bf16[32,24,3840]{2,1,0:T(8,...) while((s32[]{:T(128)}, f32[16,4,96,96]{3,2,1,0:T(8,128)}, f32[16,4,96,192]{3,2,1,0:T(8,128)}, ...), condition=%wide.region_2.3_spmd, body=%wide.region_1.2_spmd.sunk | while | flops 853771392 | bytes 50735296 | solution.py:67
  196.1 7.8 %gather_fusion.1 = bf16[16,48,3840]{2,1,0:T(8,128)(2,1)} fusion(bf16[32,48,3840]{2,1,0:T(8,128)(2,1)} %get-tuple-element.114, s32[1024]{0:T(1024)S(1)} %pad_clamp_fusion.4), kind=kCustom, calls=%fused_computation.1.clone.1 | custom fusion | bytes 11796544 | tf_op jit(solution)/shard_map/while/body/eval_jaxpr/jit(_take)/gather | solution.py:56
  211.8 5.0 gather_fusion
  219.1 7.8 %gather_fusion.1 = bf16[16,48,3840]{2,1,0:T(8,128)(2,1)} fusion(bf16[32,48,3840]{2,1,0:T(8,128)(2,1)} %get-tuple-element.114, s32[1024]{0:T(1024)S(1)} %pad_clamp_fusion.4), kind=kCustom, calls=%fused_computation.1.clone.1 | custom fusion | bytes 11796544 | tf_op jit(solution)/shard_map/while/body/eval_jaxpr/jit(_take)/gather | solution.py:56
  234.9 5.0 gather_fusion
  242.2 7.8 %gather_fusion.1 = bf16[16,48,3840]{2,1,0:T(8,128)(2,1)} fusion(bf16[32,48,3840]{2,1,0:T(8,128)(2,1)} %get-tuple-element.114, s32[1024]{0:T(1024)S(1)} %pad_clamp_fusion.4), kind=kCustom, calls=%fused_computation.1.clone.1 | custom fusion | bytes 11796544 | tf_op jit(solution)/shard_map/while/body/eval_jaxpr/jit(_take)/gather | solution.py:56
  265.3 7.8 %gather_fusion.1 = bf16[16,48,3840]{2,1,0:T(8,128)(2,1)} fusion(bf16[32,48,3840]{2,1,0:T(8,128)(2,1)} %get-tuple-element.114, s32[1024]{0:T(1024)S(1)} %pad_clamp_fusion.4), kind=kCustom, calls=%fused_computation.1.clone.1 | custom fusion | bytes 11796544 | tf_op jit(solution)/shard_map/while/body/eval_jaxpr/jit(_take)/gather | solution.py:56
  280.9 5.0 gather_fusion
  288.3 7.8 %gather_fusion.1 = bf16[16,48,3840]{2,1,0:T(8,128)(2,1)} fusion(bf16[32,48,3840]{2,1,0:T(8,128)(2,1)} %get-tuple-element.114, s32[1024]{0:T(1024)S(1)} %pad_clamp_fusion.4), kind=kCustom, calls=%fused_computation.1.clone.1 | custom fusion | bytes 11796544 | tf_op jit(solution)/shard_map/while/body/eval_jaxpr/jit(_take)/gather | solution.py:56
  304.0 5.0 gather_fusion
  311.3 7.8 %gather_fusion.1 = bf16[16,48,3840]{2,1,0:T(8,128)(2,1)} fusion(bf16[32,48,3840]{2,1,0:T(8,128)(2,1)} %get-tuple-element.114, s32[1024]{0:T(1024)S(1)} %pad_clamp_fusion.4), kind=kCustom, calls=%fused_computation.1.clone.1 | custom fusion | bytes 11796544 | tf_op jit(solution)/shard_map/while/body/eval_jaxpr/jit(_take)/gather | solution.py:56
  334.4 7.8 %gather_fusion.1 = bf16[16,48,3840]{2,1,0:T(8,128)(2,1)} fusion(bf16[32,48,3840]{2,1,0:T(8,128)(2,1)} %get-tuple-element.114, s32[1024]{0:T(1024)S(1)} %pad_clamp_fusion.4), kind=kCustom, calls=%fused_computation.1.clone.1 | custom fusion | bytes 11796544 | tf_op jit(solution)/shard_map/while/body/eval_jaxpr/jit(_take)/gather | solution.py:56
  357.4 7.8 %gather_fusion.1 = bf16[16,48,3840]{2,1,0:T(8,128)(2,1)} fusion(bf16[32,48,3840]{2,1,0:T(8,128)(2,1)} %get-tuple-element.114, s32[1024]{0:T(1024)S(1)} %pad_clamp_fusion.4), kind=kCustom, calls=%fused_computation.1.clone.1 | custom fusion | bytes 11796544 | tf_op jit(solution)/shard_map/while/body/eval_jaxpr/jit(_take)/gather | solution.py:56
  380.5 7.8 %gather_fusion.1 = bf16[16,48,3840]{2,1,0:T(8,128)(2,1)} fusion(bf16[32,48,3840]{2,1,0:T(8,128)(2,1)} %get-tuple-element.114, s32[1024]{0:T(1024)S(1)} %pad_clamp_fusion.4), kind=kCustom, calls=%fused_computation.1.clone.1 | custom fusion | bytes 11796544 | tf_op jit(solution)/shard_map/while/body/eval_jaxpr/jit(_take)/gather | solution.py:56
  403.5 7.8 %gather_fusion.1 = bf16[16,48,3840]{2,1,0:T(8,128)(2,1)} fusion(bf16[32,48,3840]{2,1,0:T(8,128)(2,1)} %get-tuple-element.114, s32[1024]{0:T(1024)S(1)} %pad_clamp_fusion.4), kind=kCustom, calls=%fused_computation.1.clone.1 | custom fusion | bytes 11796544 | tf_op jit(solution)/shard_map/while/body/eval_jaxpr/jit(_take)/gather | solution.py:56
  426.6 7.8 %gather_fusion.1 = bf16[16,48,3840]{2,1,0:T(8,128)(2,1)} fusion(bf16[32,48,3840]{2,1,0:T(8,128)(2,1)} %get-tuple-element.114, s32[1024]{0:T(1024)S(1)} %pad_clamp_fusion.4), kind=kCustom, calls=%fused_computation.1.clone.1 | custom fusion | bytes 11796544 | tf_op jit(solution)/shard_map/while/body/eval_jaxpr/jit(_take)/gather | solution.py:56
  449.6 7.8 %gather_fusion.1 = bf16[16,48,3840]{2,1,0:T(8,128)(2,1)} fusion(bf16[32,48,3840]{2,1,0:T(8,128)(2,1)} %get-tuple-element.114, s32[1024]{0:T(1024)S(1)} %pad_clamp_fusion.4), kind=kCustom, calls=%fused_computation.1.clone.1 | custom fusion | bytes 11796544 | tf_op jit(solution)/shard_map/while/body/eval_jaxpr/jit(_take)/gather | solution.py:56
  472.6 7.8 %gather_fusion.1 = bf16[16,48,3840]{2,1,0:T(8,128)(2,1)} fusion(bf16[32,48,3840]{2,1,0:T(8,128)(2,1)} %get-tuple-element.114, s32[1024]{0:T(1024)S(1)} %pad_clamp_fusion.4), kind=kCustom, calls=%fused_computation.1.clone.1 | custom fusion | bytes 11796544 | tf_op jit(solution)/shard_map/while/body/eval_jaxpr/jit(_take)/gather | solution.py:56
  495.7 7.8 %gather_fusion.1 = bf16[16,48,3840]{2,1,0:T(8,128)(2,1)} fusion(bf16[32,48,3840]{2,1,0:T(8,128)(2,1)} %get-tuple-element.114, s32[1024]{0:T(1024)S(1)} %pad_clamp_fusion.4), kind=kCustom, calls=%fused_computation.1.clone.1 | custom fusion | bytes 11796544 | tf_op jit(solution)/shard_map/while/body/eval_jaxpr/jit(_take)/gather | solution.py:56
  518.7 7.8 %gather_fusion.1 = bf16[16,48,3840]{2,1,0:T(8,128)(2,1)} fusion(bf16[32,48,3840]{2,1,0:T(8,128)(2,1)} %get-tuple-element.114, s32[1024]{0:T(1024)S(1)} %pad_clamp_fusion.4), kind=kCustom, calls=%fused_computation.1.clone.1 | custom fusion | bytes 11796544 | tf_op jit(solution)/shard_map/while/body/eval_jaxpr/jit(_take)/gather | solution.py:56
  541.8 7.8 %gather_fusion.1 = bf16[16,48,3840]{2,1,0:T(8,128)(2,1)} fusion(bf16[32,48,3840]{2,1,0:T(8,128)(2,1)} %get-tuple-element.114, s32[1024]{0:T(1024)S(1)} %pad_clamp_fusion.4), kind=kCustom, calls=%fused_computation.1.clone.1 | custom fusion | bytes 11796544 | tf_op jit(solution)/shard_map/while/body/eval_jaxpr/jit(_take)/gather | solution.py:56
  562.5 6.1 pad_maximum_fusion
  568.7 87.8 %reduce-scatter.2.cloned.1.call-done = f32[64,24,288]{2,1,0:T(8,128)} async-done(((f32[64,96,288]{2,1,0:T(8,128)}), f32[64,24,288]{2,1,0:T(8,128)}) %reduce-scatter.2.cloned.1.call-update) | async-done | bytes 1769488 | tf_op jit(solution)/shard_map/reduce_scatter | solution.py:14
  660.1 22.5 %all-gather = bf16[32,2,48]{2,1,0:T(2,128)(2,1)S(1)} all-gather(bf16[1,2,48]{2,1,0:T(2,128)(2,1)S(1)} %bitcast.64), channel_id=1, replica_groups=mesh['atom'=32,'aux'=4] {'atom'}, dimensions={0}, use_global_device_ids=true | all-gather | bytes 6336 | tf_op jit(solution)/shard_map/all_gather | solution.py:41
  684.5 41.0 %all-gather.9.cloned.1.call-done = f32[64,96,192]{2,1,0:T(8,128)} async-done(((f32[64,24,192]{2,1,0:T(8,128)}), f32[64,96,192]{2,1,0:T(8,128)}) %all-gather.9.cloned.1.call-update) | async-done | bytes 4718608 | tf_op jit(solution)/shard_map/all_gather | solution.py:84
  725.4 8.0 %fusion.7 = f32[64,24,96]{2,1,0:T(8,128)} fusion(f32[64,96,192]{2,1,0:T(8,128)} %all-gather.9.cloned.1.call-done, f32[64,24,288]{2,1,0:T(8,128)S(1)} %copy-done.1, f32[64,192]{1,0:T(8,128)S(1)} %select_convert_fusion), kind=kOutput, calls=%fused_computation.27 | convolution fusion | flops 340180992 | bytes 7127040 | tf_op jit(solution)/shard_map/pix,pjx->pij/dot_general | solution.py:85
  (246 shorter events, 237.7 us)
Async XLA Ops:
  6.5 67.7 %all-gather.5.cloned.1.call-start = ((), (), s32[]{:S(2)}) async-start(), calls=%async_computation.1 | async-start | bytes 12165120 | tf_op jit(solution)/shard_map/all_gather | solution.py:39
  7.3 157.0 %all-gather.7.cloned.1.call-start = ((), (), s32[]{:S(2)}) async-start(), calls=%async_computation.2 | async-start | bytes 24330240 | tf_op jit(solution)/shard_map/all_gather | solution.py:40
  8.0 648.6 %reduce-scatter.2.cloned.1.call-start = ((), (), s32[]{:S(2)}) async-start(), calls=%async_computation.3 | async-start | bytes 11796480 | tf_op jit(solution)/shard_map/reduce_scatter | solution.py:14
  557.3 3.7 copy-start
  568.6 91.5 %copy-start.3 = (bf16[2,48]{1,0:T(2,128)(2,1)S(1)}, bf16[2,48]{1,0:T(2,128)(2,1)}, u32[]{:S(2)}) copy-start(bf16[2,48]{1,0:T(2,128)(2,1)} %param.10) | copy-start | bytes 580
  568.7 115.7 %copy-start.2 = (s32[64,4]{0,1:T(4,128)S(1)}, s32[64,4]{0,1:T(4,128)}, u32[]{:S(2)}) copy-start(s32[64,4]{0,1:T(4,128)} %param.11) | copy-start | bytes 3076
  568.7 156.8 %all-gather.9.cloned.1.call-start = ((), (), s32[]{:S(2)}) async-start(), calls=%async_computation.4 | async-start | bytes 7864320 | tf_op jit(solution)/shard_map/all_gather | solution.py:84
  656.6 68.9 %copy-start.1 = (f32[64,24,288]{2,1,0:T(8,128)S(1)}, f32[64,24,288]{2,1,0:T(8,128)}, u32[]{:S(2)}) copy-start(f32[64,24,288]{2,1,0:T(8,128)} %reduce-scatter.2.cloned.1.call-done) | copy-start | bytes 5308420
Sparse Core Ops, SparseCore 0:
  9.6 64.6 all-gather.4
  76.5 87.6 all-gather.6
  568.8 87.7 reduce-scatter.1
  660.1 65.2 all-gather.8
where the time goes:
time: 743 us; the launch traced here: 740 us
  waiting for transfers between devices  270 us (36%)
  local copies, waits for them, and re-layouts  241 us (32%)
  other arithmetic  115 us (15%)
  matrix products  77.5 us (10%)
  blocking collectives  22.5 us (3%)
  between operations  13.3 us (2%)
    gather x16, local copies, waits for them, and re-layouts, pair_products(): jnp.take(slot_cabs, slots.reshape(-1), axis=0)  125 us
    reduce_scatter x1, waiting for transfers between devices, sent_together(): lax.psum_scatter(both, axis, scatter_dimension=dim, tiled=True)  87.8 us
    gather x16, local copies, waits for them, and re-layouts, pair_products(): jnp.take(slot_pao, slots.reshape(-1), axis=0)  80.2 us
    all_gather x1, waiting for transfers between devices, shards(): lax.all_gather(cabs_blocks, 'atom', axis=0, tiled=True)  76.2 us
    all_gather x1, waiting for transfers between devices, shards(): lax.all_gather(pao_blocks, 'atom', axis=0, tiled=True)  63.6 us
    select_n x16, other arithmetic, pair_products(): jnp.take(slot_cabs, slots.reshape(-1), axis=0)  52.2 us
    dot_general x16, matrix products, pair_products(): jnp.einsum('pia,pja->pij', rows_pao, rows_cabs, preferred_element_type=jn...  43.9 us
    all_gather x1, waiting for transfers between devices, shards(): coupling_full = lax.all_gather(coupling_rows, 'aux', axis=1, tiled=True)  41 us
  transfers between devices with their start and end apart: 4, of which 4 were waited for; matrix products, arithmetic and copies ran while one was open for 2% of the time, Pallas kernels for 0%

commit v1 on v0

--- a/solution.py
+++ b/solution.py
@@ -36,7 +36,10 @@
     wanted = jnp.max(jnp.where(matches, flat_blocks[:, None], -1), axis=0)
     every_pao, every_cabs, every_weight = collect(
         (
-            lax.all_gather(pao_blocks, "atom", axis=0, tiled=True),
+            jnp.concatenate(
+                lax.all_to_all(jnp.stack([pao_blocks] * lax.axis_size("atom")), "atom", 0, 0),
+                axis=0,
+            ),
             lax.all_gather(cabs_blocks, "atom", axis=0, tiled=True),
             lax.all_gather(cabs_weight, "atom", axis=0, tiled=True),
         )

time: 743 us -> 847 us (1.14)
  waiting for transfers between devices: 270 us -> 360 us
  starting transfers between devices: 0.12 us -> 9.86 us
    all_to_all x0 -> x1, waiting for transfers between devices: none -> 175 us  [shards(): lax.all_to_all(jnp.stack([pao_blocks] * lax.axis_size('atom')), 'atom', 0...]
    all_gather x1, waiting for transfers between devices: 76.2 us -> 11.3 us  [shards(): lax.all_gather(cabs_blocks, 'atom', axis=0, tiled=True)]
    all_gather x1 -> x0, waiting for transfers between devices: 63.6 us -> none  [shards(): lax.all_gather(pao_blocks, 'atom', axis=0, tiled=True)]
    reduce_scatter x1, waiting for transfers between devices: 87.8 us -> 131 us  [sent_together(): lax.psum_scatter(both, axis, scatter_dimension=dim, tiled=True)]
    all_to_all x0 -> x1, starting transfers between devices: none -> 9.77 us  [shards(): lax.all_to_all(jnp.stack([pao_blocks] * lax.axis_size('atom')), 'atom', 0...]
  transfers between devices with their start and end apart: 4 -> 4, of which waited for: 4 -> 4; matrix products, arithmetic and copies ran while one was open for 2% -> 3% of each run, Pallas kernels for 0% -> 0%
where the time goes in v1:
time: 847 us; the launch traced here: 845 us
  waiting for transfers between devices  360 us (43%)
  local copies, waits for them, and re-layouts  248 us (29%)
  other arithmetic  114 us (13%)
  matrix products  77.4 us (9%)
  blocking collectives  22.5 us (3%)
  between operations  13.3 us (2%)
  starting transfers between devices  9.86 us (1%)
    all_to_all x1, waiting for transfers between devices, shards(): lax.all_to_all(jnp.stack([pao_blocks] * lax.axis_size('atom')), 'atom', 0...  175 us
    reduce_scatter x1, waiting for transfers between devices, sent_together(): lax.psum_scatter(both, axis, scatter_dimension=dim, tiled=True)  131 us
    gather x16, local copies, waits for them, and re-layouts, pair_products(): jnp.take(slot_cabs, slots.reshape(-1), axis=0)  126 us
    gather x16, local copies, waits for them, and re-layouts, pair_products(): jnp.take(slot_pao, slots.reshape(-1), axis=0)  80.5 us
    select_n x16, other arithmetic, pair_products(): jnp.take(slot_cabs, slots.reshape(-1), axis=0)  52.2 us
    dot_general x16, matrix products, pair_products(): jnp.einsum('pia,pja->pij', rows_pao, rows_cabs, preferred_element_type=jn...  43.9 us
    all_gather x1, waiting for transfers between devices, shards(): coupling_full = lax.all_gather(coupling_rows, 'aux', axis=1, tiled=True)  41 us
    select_n x32, other arithmetic, pair_products(): jnp.take(slot_pao, slots.reshape(-1), axis=0)  34.6 us
  transfers between devices with their start and end apart: 4, of which 4 were waited for; matrix products, arithmetic and copies ran while one was open for 3% of the time, Pallas kernels for 0%

profile of v1, /device:TPU:1, one launch (start us, length us, event | category | flops | bytes accessed | tf_op | source)
XLA Modules:
  0.0 844.6 jit_solution(15673859555926879150)
XLA Ops:
  7.3 6.1 stack.2
  13.3 9.8 %all-to-all-start = ((bf16[32,2,24,3840]{3,2,1,0:T(8,128)(2,1)}), bf16[32,2,24,3840]{3,2,1,0:T(8,128)(2,1)}, u32[]{:S(2)}, u32[]{:S(2)}) async-start(bf16[32,2,24,3840]{3,2,1,0:T(8,128)(2,1)} %stack.2), calls=%async_computation | async-start | bytes 23592960 | tf_op jit(solution)/shard_map/all_to_all | solution.py:40
  23.8 175.5 %all-to-all-done = bf16[32,2,24,3840]{3,2,1,0:T(8,128)(2,1)} async-done(((bf16[32,2,24,3840]{3,2,1,0:T(8,128)(2,1)}), bf16[32,2,24,3840]{3,2,1,0:T(8,128)(2,1)}, u32[]{:S(2)}, u32[]{:S(2)}) %all-to-all-start) | async-done | bytes 11796512 | tf_op jit(solution)/shard_map/all_to_all | solution.py:40
  199.3 8.2 gather_fusion.2
  207.5 5.9 broadcast_select_fusion.1
  213.4 11.3 %all-gather.4.cloned.1.call-done = bf16[64,48,3840]{2,1,0:T(8,128)(2,1)} async-done(((bf16[2,48,3840]{2,1,0:T(8,128)(2,1)}), bf16[64,48,3840]{2,1,0:T(8,128)(2,1)}) %all-gather.4.cloned.1.call-update) | async-done | bytes 23592976 | tf_op jit(solution)/shard_map/all_gather | solution.py:43
  224.7 14.1 %gather_fusion.3 = bf16[32,48,3840]{2,1,0:T(8,128)(2,1)} fusion(bf16[64,48,3840]{2,1,0:T(8,128)(2,1)} %all-gather.4.cloned.1.call-done, s32[1024]{0:T(1024)S(1)} %pad_clamp_fusion.2), kind=kCustom, calls=%fused_computation.3 | custom fusion | bytes 23593088 | tf_op jit(solution)/shard_map/jit(_take)/gather | solution.py:49
  238.8 10.3 %broadcast_select_fusion = bf16[32,48,3840]{2,1,0:T(8,128)(2,1)} fusion(bf16[32,48,3840]{2,1,0:T(8,128)(2,1)} %gather_fusion.3, pred[32]{0:T(512)(128)(4,1)S(1)} %broadcast_compare_fusion), kind=kLoop, calls=%fused_computation.18 | loop fusion | flops 5898240 | bytes 23592992 | tf_op jit(solution)/shard_map/jit(_take)/select_n | solution.py:49
  249.1 369.4 %while.12 = (s32[]{:T(128)}, f32[16,4,96,96]{3,2,1,0:T(8,128)}, f32[16,4,96,192]{3,2,1,0:T(8,128)}, s32[16,4,4]{2,1,0:T(4,128)S(1)}, bf16[32,24,3840]{2,1,0:T(8,...) while((s32[]{:T(128)}, f32[16,4,96,96]{3,2,1,0:T(8,128)}, f32[16,4,96,192]{3,2,1,0:T(8,128)}, ...), condition=%wide.region_2.3_spmd, body=%wide.region_1.2_spmd.sunk | while | flops 853771392 | bytes 50735296 | solution.py:70
  256.6 7.8 gather_fusion.1
  279.7 7.8 gather_fusion.1
  302.8 7.8 gather_fusion.1
  325.9 7.8 gather_fusion.1
  341.6 5.0 gather_fusion
  349.0 7.8 gather_fusion.1
  364.7 5.0 gather_fusion
  372.1 7.8 gather_fusion.1
  395.2 7.8 gather_fusion.1
  418.3 7.8 gather_fusion.1
  441.3 7.8 gather_fusion.1
  464.4 7.8 gather_fusion.1
  487.5 7.8 gather_fusion.1
  510.6 7.8 gather_fusion.1
  533.7 7.8 gather_fusion.1
  556.7 7.8 gather_fusion.1
  579.8 7.8 gather_fusion.1
  602.9 7.8 gather_fusion.1
  623.6 6.1 pad_maximum_fusion
  629.9 131.3 %reduce-scatter.2.cloned.1.call-done = f32[64,24,288]{2,1,0:T(8,128)} async-done(((f32[64,96,288]{2,1,0:T(8,128)}), f32[64,24,288]{2,1,0:T(8,128)}) %reduce-scatter.2.cloned.1.call-update) | async-done | bytes 1769488 | tf_op jit(solution)/shard_map/reduce_scatter | solution.py:14
  764.8 22.5 %all-gather = bf16[32,2,48]{2,1,0:T(2,128)(2,1)S(1)} all-gather(bf16[1,2,48]{2,1,0:T(2,128)(2,1)S(1)} %bitcast.65), channel_id=1, replica_groups=mesh['atom'=32,'aux'=4] {'atom'}, dimensions={0}, use_global_device_ids=true | all-gather | bytes 6336 | tf_op jit(solution)/shard_map/all_gather | solution.py:44
  789.1 41.0 %all-gather.6.cloned.1.call-done = f32[64,96,192]{2,1,0:T(8,128)} async-done(((f32[64,24,192]{2,1,0:T(8,128)}), f32[64,96,192]{2,1,0:T(8,128)}) %all-gather.6.cloned.1.call-update) | async-done | bytes 4718608 | tf_op jit(solution)/shard_map/all_gather | solution.py:87
  830.0 8.0 fusion.7
  (250 shorter events, 245.2 us)
Async XLA Ops:
  6.5 218.2 %all-gather.4.cloned.1.call-start = ((), (), s32[]{:S(2)}) async-start(), calls=%async_computation.2 | async-start | bytes 24330240 | tf_op jit(solution)/shard_map/all_gather | solution.py:43
  13.3 9.9 %copy-start.2 = (s32[64,4]{0,1:T(4,128)S(1)}, s32[64,4]{0,1:T(4,128)}, u32[]{:S(2)}) copy-start(s32[64,4]{0,1:T(4,128)} %param.11) | copy-start | bytes 3076
  13.3 10.2 %copy-start.3 = (s32[64]{0:T(128)S(1)}, s32[64]{0:T(128)}, u32[]{:S(2)}) copy-start(s32[64]{0:T(128)} %param.12) | copy-start | bytes 772
  13.3 10.4 %copy-start.4 = (s32[64]{0:T(128)S(1)}, s32[64]{0:T(128)}, u32[]{:S(2)}) copy-start(s32[64]{0:T(128)} %param.13) | copy-start | bytes 772
  13.3 185.9 %all-to-all-start = ((bf16[32,2,24,3840]{3,2,1,0:T(8,128)(2,1)}), bf16[32,2,24,3840]{3,2,1,0:T(8,128)(2,1)}, u32[]{:S(2)}, u32[]{:S(2)}) async-start(bf16[32,2,24,3840]{3,2,1,0:T(8,128)(2,1)} %stack.2), calls=%async_computation | async-start | bytes 23592960 | tf_op jit(solution)/shard_map/all_to_all | solution.py:40
  23.1 738.1 %reduce-scatter.2.cloned.1.call-start = ((), (), s32[]{:S(2)}) async-start(), calls=%async_computation.3 | async-start | bytes 11796480 | tf_op jit(solution)/shard_map/reduce_scatter | solution.py:14
  618.5 3.7 copy-start
  629.8 135.0 %copy-start.5 = (bf16[2,48]{1,0:T(2,128)(2,1)S(1)}, bf16[2,48]{1,0:T(2,128)(2,1)}, u32[]{:S(2)}) copy-start(bf16[2,48]{1,0:T(2,128)(2,1)} %param.10) | copy-start | bytes 580
  629.8 200.2 %all-gather.6.cloned.1.call-start = ((), (), s32[]{:S(2)}) async-start(), calls=%async_computation.4 | async-start | bytes 7864320 | tf_op jit(solution)/shard_map/all_gather | solution.py:87
  761.2 68.9 %copy-start.1 = (f32[64,24,288]{2,1,0:T(8,128)S(1)}, f32[64,24,288]{2,1,0:T(8,128)}, u32[]{:S(2)}) copy-start(f32[64,24,288]{2,1,0:T(8,128)} %reduce-scatter.2.cloned.1.call-done) | copy-start | bytes 5308420
Sparse Core Ops, SparseCore 0:
  9.6 215.0 all-gather.3
  629.9 131.2 reduce-scatter.1
  764.8 65.2 all-gather.5
